TPU v7x, 32 devices: a whole 2x2x4 slice. The times are simulated.
32 devices in a mesh: section: 8 (over z, core), board: 4 (over y, x).
Axes of the slice: x: 2, y: 2, z: 4, core: 2. Of those that a mesh axis runs over, the one named last changes fastest.
Arguments:
- root_reach: float32 [2, 8, 1326], replicated, may hold values from 0.05 to 1
- frontier_value: float32 [2, 8, 1326], replicated, may hold values from -60 to 60
- regret_stop: float32 [8, 16, 8, 1326], P('section', 'board'), may hold values from 1 to 30
- regret_go: float32 [8, 16, 8, 1326], P('section', 'board'), may hold values from 1 to 30
- board_live: int32 [16], P('board'), may hold values from 0 to 1, as said below
- board_cards: int32 [16, 5], P('board'), may hold values from 0 to 51, as said below
- hand_rank: int32 [16, 1326], P('board'), may hold values from 0 to 1325
Outputs:
- new_stop: float32 [8, 16, 8, 1326], P('section', 'board')
- new_go: float32 [8, 16, 8, 1326], P('section', 'board')
- section_values: float32 [8, 2, 8, 1326], P('section')
Inputs may be any that keep to these rules, and one draw needn't show every extreme that they name: `board_live`: 0 or 1; among each device's 4 slots the first one is always 1. `board_cards`: a slot's 5 cards are distinct. `hand_rank`: equal values tie.
All inputs are finite; a program needn't handle non-finite values.
Results may differ from a plain program's by a relative error of at most 0.0008.
Values sent between devices are 32-bit elements; how exact they have to be, the bound alone decides.
A program may use at most 64 MiB of HBM per device.

v0:
```python
import jax
import jax.numpy as jnp
import numpy as np
from jax import lax
from jax.sharding import PartitionSpec as P

CARDS = 52


def free_pairs():
    first, second = np.triu_indices(CARDS, 1)
    first = jnp.asarray(first.astype(np.int32))
    second = jnp.asarray(second.astype(np.int32))
    shared = (
        (first[:, None] == first[None, :])
        | (first[:, None] == second[None, :])
        | (second[:, None] == first[None, :])
        | (second[:, None] == second[None, :])
    )
    return jnp.where(shared, 0.0, 1.0).astype(jnp.bfloat16)


def board_masks(board_cards):
    first, second = np.triu_indices(CARDS, 1)
    first = jnp.asarray(first.astype(np.int32))
    second = jnp.asarray(second.astype(np.int32))
    hits = (board_cards[:, :, None] == first[None, None, :]) | (
        board_cards[:, :, None] == second[None, None, :]
    )
    return jnp.where(jnp.any(hits, axis=1), 0.0, 1.0).astype(jnp.float32)


def showdown(reach_one, stop_weight, mask_row, rank_row, disjoint):
    leaf_reach = (reach_one * stop_weight).astype(jnp.bfloat16)
    mask_half = mask_row.astype(jnp.bfloat16)
    payoff = (
        jnp.sign(rank_row[:, None] - rank_row[None, :]).astype(jnp.bfloat16)
        * disjoint
        * mask_half[:, None]
        * mask_half[None, :]
    )
    flipped = leaf_reach[::-1].reshape(-1, leaf_reach.shape[-1])
    result = jnp.einsum("rk,hk->rh", flipped, payoff, preferred_element_type=jnp.float32)
    return result.reshape(leaf_reach.shape)


def local(root_reach, frontier_value, regret_stop, regret_go, board_live, board_cards, hand_rank):
    section_idx = lax.axis_index("section")
    players = jnp.arange(2)[:, None, None]
    acting = players == section_idx % 2
    masks = board_masks(board_cards)
    alive = board_live > 0
    alive_weight = alive.astype(jnp.float32)
    stop_now = regret_stop[0]
    go_now = regret_go[0]
    regret_sum = stop_now + go_now
    stop_prob = stop_now / regret_sum
    go_prob = go_now / regret_sum
    factor = jnp.where(acting[None], go_prob[:, None], 1.0)
    stop_weight = jnp.where(acting[None], stop_prob[:, None], 1.0)
    root_masked = root_reach[None] * masks[:, None, None, :]
    factor_all = lax.all_gather(factor[None], "section", axis=0, tiled=True)
    levels = jnp.arange(factor_all.shape[0])[:, None, None, None, None]
    reach_now = root_masked * jnp.prod(jnp.where(levels < section_idx, factor_all, 1.0), axis=0)
    disjoint = free_pairs()
    leaf_list = []
    for slot in range(masks.shape[0]):
        leaf_one = showdown(
            reach_now[slot], stop_weight[slot], masks[slot], hand_rank[slot], disjoint
        )
        leaf_list.append(leaf_one)
    leaf_values = jnp.stack(leaf_list)
    weighted = stop_weight * leaf_values
    frontier_masked = frontier_value[None] * masks[:, None, None, :]
    leaf_all = lax.all_gather(weighted[None], "section", axis=0, tiled=True)
    section_total = leaf_all.shape[0]

    def climb(position, carried):
        level_now = section_total - 1 - position
        updated = leaf_all[level_now] + factor_all[level_now] * carried
        return jnp.where(level_now > section_idx, updated, carried)

    value_next = lax.fori_loop(0, section_total, climb, frontier_masked)
    node_value = weighted + factor * value_next
    section_part = jnp.sum(alive_weight[:, None, None, None] * node_value, axis=0)
    live_part = jnp.sum(alive_weight)
    section_sum, live_total = lax.psum((section_part, live_part), "board")
    section_value = section_sum / live_total
    own_next = jnp.sum(jnp.where(acting[None], value_next, 0.0), axis=1)
    own_leaf = jnp.sum(jnp.where(acting[None], leaf_values, 0.0), axis=1)
    gap = own_leaf - own_next
    keep_slot = alive[:, None, None]
    new_stop = jnp.where(keep_slot, jnp.maximum(stop_now + go_prob * gap, 0.0), stop_now)
    new_go = jnp.where(keep_slot, jnp.maximum(go_now - stop_prob * gap, 0.0), go_now)
    return (new_stop[None], new_go[None], section_value[None])


def solution(mesh):
    return jax.shard_map(
        local,
        mesh=mesh,
        in_specs=(
            P(),
            P(),
            P("section", "board", None, None),
            P("section", "board", None, None),
            P("board"),
            P("board", None),
            P("board", None),
        ),
        out_specs=(
            P("section", "board", None, None),
            P("section", "board", None, None),
            P("section", None, None, None),
        ),
        check_vma=False,
    )
```

profile of v0, /device:TPU:0, one launch (start us, length us, event | category | flops | bytes accessed | tf_op | source)
XLA Modules:
  0.0 163.7 jit_solution(3219703104629716634)
XLA Ops:
  7.3 1.0 add_divide_fusion.1
  8.3 0.8 broadcast_select_fusion.1
  9.2 0.8 copy.14
  10.0 0.8 or_reduce_fusion
  10.8 0.1 fusion.53
  10.9 0.9 slice_reduce_fusion.3
  11.9 0.1 broadcast_select_fusion
  12.0 36.4 %all-gather.3.cloned.1.call-done = f32[8,4,2,8,1326]{4,3,2,1,0:T(8,128)} async-done(((f32[1,4,2,8,1326]{4,3,2,1,0:T(8,128)}), f32[8,4,2,8,1326]{4,3,2,1,0:T(8,128)}) %all-gather.3.cloned.1.call-update) | async-done | bytes 2715664 | tf_op jit(solution)/shard_map/all_gather | solution.py:62
  48.3 2.1 %select_reduce_fusion = f32[4,2,8,1326]{3,2,1,0:T(8,128)S(1)} fusion(f32[8,4,2,8,1326]{4,3,2,1,0:T(8,128)} %all-gather.3.cloned.1.call-done, pred[8]{0:T(512)(128)(4,1)S(1)} %iota_compare_fusion), kind=kLoop, calls=%fused_computation.28 | loop fusion | flops 1272960 | bytes 3055112 | tf_op jit(solution)/shard_map/reduce_prod | solution.py:64
  50.5 0.1 multiply_multiply_fusion
  50.6 0.1 fusion.46
  50.7 3.7 %fusion.24 = f32[2,8,1326]{2,1,0:T(8,128)S(1)} fusion(bf16[2,8,1326]{2,1,0:T(8,128)(2,1)S(1)} %rev.12, s32[1326]{0:T(1024)S(1)} %get-tuple-element.143, s32[1326]{0:T(1024)S(1)} %copy-done.5, s32[1326]{0:T(1024)S(1)} %copy-done.4, bf16[1326]{0:T(1024)(128)(2,1)S(1)} %get-tuple-element.139), kind=kOutput, calls=%fused_computation.27 | convolution fusion | flops 91430352 | bytes 145860 | tf_op jit(solution)/shard_map/rk,hk->rh/dot_general | solution.py:43
  54.4 3.7 %fusion.22 = f32[2,8,1326]{2,1,0:T(8,128)S(1)} fusion(bf16[2,8,1326]{2,1,0:T(8,128)(2,1)S(1)} %rev.13, s32[1326]{0:T(1024)S(1)} %get-tuple-element.144, s32[1326]{0:T(1024)S(1)} %copy-done.5, s32[1326]{0:T(1024)S(1)} %copy-done.4, bf16[1326]{0:T(1024)(128)(2,1)S(1)} %get-tuple-element.142), kind=kOutput, calls=%fused_computation.26 | convolution fusion | flops 91430352 | bytes 145860 | tf_op jit(solution)/shard_map/rk,hk->rh/dot_general | solution.py:43
  58.1 3.7 %fusion.20 = f32[2,8,1326]{2,1,0:T(8,128)S(1)} fusion(bf16[2,8,1326]{2,1,0:T(8,128)(2,1)S(1)} %rev.14, s32[1326]{0:T(1024)S(1)} %get-tuple-element.146, s32[1326]{0:T(1024)S(1)} %copy-done.5, s32[1326]{0:T(1024)S(1)} %copy-done.4, bf16[1326]{0:T(1024)(128)(2,1)S(1)} %get-tuple-element.141), kind=kOutput, calls=%fused_computation.25 | convolution fusion | flops 91430352 | bytes 145860 | tf_op jit(solution)/shard_map/rk,hk->rh/dot_general | solution.py:43
  61.8 3.9 %fusion.18 = f32[2,8,1326]{2,1,0:T(8,128)S(1)} fusion(bf16[2,8,1326]{2,1,0:T(8,128)(2,1)S(1)} %rev.15, s32[1326]{0:T(1024)S(1)} %get-tuple-element.145, s32[1326]{0:T(1024)S(1)} %copy-done.5, s32[1326]{0:T(1024)S(1)} %copy-done.4, bf16[1326]{0:T(1024)(128)(2,1)S(1)} %get-tuple-element.140), kind=kOutput, calls=%fused_computation.24 | convolution fusion | flops 91430352 | bytes 145860 | tf_op jit(solution)/shard_map/rk,hk->rh/dot_general | solution.py:43
  65.7 0.8 maximum_multiply_fusion
  66.6 0.6 convert_reduce_fusion
  67.2 10.5 %psum.15 = f32[]{:T(128)} all-reduce(f32[]{:T(128)} %convert_reduce_fusion), channel_id=1, replica_groups=mesh['section'=8,'board'=4] {'board'}, use_global_device_ids=true, to_apply=%region_9.10 | all-reduce | flops 1 | bytes 8 | tf_op jit(solution)/shard_map/psum | solution.py:87
  77.8 23.9 %all-gather.5.cloned.1.call-done = f32[8,4,2,8,1326]{4,3,2,1,0:T(8,128)} async-done(((f32[1,4,2,8,1326]{4,3,2,1,0:T(8,128)}), f32[8,4,2,8,1326]{4,3,2,1,0:T(8,128)}) %all-gather.5.cloned.1.call-update) | async-done | bytes 2715664 | tf_op jit(solution)/shard_map/all_gather | solution.py:75
  101.7 11.1 %while.15 = (s32[]{:T(128)}, f32[4,2,8,1326]{3,2,1,0:T(8,128)S(1)}, s32[]{:T(128)}, f32[8,4,2,8,1326]{4,3,2,1,0:T(8,128)}, f32[8,4,2,8,1326]{4,3,2,1,0:T(8,128)}...) while((s32[]{:T(128)}, f32[4,2,8,1326]{3,2,1,0:T(8,128)S(1)}, s32[]{:T(128)}, ...), condition=%wide.region_4.5_spmd, body=%wide.region_3.4_spmd.sunk | while | flops 254599 | bytes 1357977 | solution.py:83
  101.7 1.4 fusion.68
  103.1 1.4 fusion.68
  104.5 1.4 fusion.68
  105.9 1.4 fusion.68
  107.3 1.4 fusion.68
  108.7 1.4 fusion.68
  110.1 1.4 fusion.68
  111.5 1.4 fusion.68
  112.8 0.9 multiply_reduce_fusion
  113.7 0.8 fusion.41
  114.6 40.3 %all-reduce.2.cloned.1.call-done = f32[2,8,1326]{2,1,0:T(8,128)} async-done(((f32[2,8,1326]{2,1,0:T(8,128)}), f32[2,8,1326]{2,1,0:T(8,128)}) %all-reduce.2.cloned.1.call-update) | async-done | bytes 84880 | tf_op jit(solution)/shard_map/psum | solution.py:87
  154.9 2.2 %divide_bitcast_fusion = f32[1,2,8,1326]{3,2,1,0:T(8,128)} fusion(f32[2,8,1326]{2,1,0:T(8,128)} %all-reduce.2.cloned.1.call-done, f32[]{:T(128)} %psum.15), kind=kLoop, calls=%fused_computation.67 | loop fusion | flops 21216 | bytes 169732 | tf_op jit(solution)/shard_map/broadcast_in_dim | solution.py:95
  (28 shorter events, 0.3 us)
Async XLA Ops:
  7.2 43.3 %copy-start.2 = (f32[2,8,1326]{2,1,0:T(8,128)S(1)}, f32[2,8,1326]{2,1,0:T(8,128)}, u32[]{:S(2)}) copy-start(f32[2,8,1326]{2,1,0:T(8,128)} %param.13) | copy-start | bytes 254596
  7.2 43.3 %copy-start.3 = (f32[2,8,1326]{2,1,0:T(8,128)S(1)}, f32[2,8,1326]{2,1,0:T(8,128)}, u32[]{:S(2)}) copy-start(f32[2,8,1326]{2,1,0:T(8,128)} %param.14) | copy-start | bytes 254596
  7.2 41.2 %all-gather.3.cloned.1.call-start = ((), (), s32[]{:S(2)}) async-start(), calls=%async_computation | async-start | bytes 3244032 | tf_op jit(solution)/shard_map/all_gather | solution.py:62
  9.2 92.5 %all-gather.5.cloned.1.call-start = ((), (), s32[]{:S(2)}) async-start(), calls=%async_computation.1 | async-start | bytes 3244032 | tf_op jit(solution)/shard_map/all_gather | solution.py:75
  12.0 38.7 %copy-start.4 = (s32[1326]{0:T(1024)S(1)}, s32[1326]{0:T(1024)}, u32[]{:S(2)}) copy-start(s32[1326]{0:T(1024)} %constant.74.clone) | copy-start | bytes 15916
  12.0 38.7 %copy-start.5 = (s32[1326]{0:T(1024)S(1)}, s32[1326]{0:T(1024)}, u32[]{:S(2)}) copy-start(s32[1326]{0:T(1024)} %constant.75.clone) | copy-start | bytes 15916
  61.8 4.8 %copy-start.6 = (s32[4]{0:T(128)S(1)}, s32[4]{0:T(128)}, u32[]{:S(2)}) copy-start(s32[4]{0:T(128)} %param.17) | copy-start | bytes 52
  66.6 88.3 %all-reduce.2.cloned.1.call-start = ((), (), s32[]{:S(2)}) async-start(), calls=%async_computation.2 | async-start | bytes 180224 | tf_op jit(solution)/shard_map/psum | solution.py:87
  101.7 12.0 %copy-start = (f32[1,4,8,1326]{3,2,1,0:T(8,128)S(1)}, f32[1,4,8,1326]{3,2,1,0:T(8,128)}, u32[]{:S(2)}) copy-start(f32[1,4,8,1326]{3,2,1,0:T(8,128)} %param.16) | copy-start | bytes 509188
  101.7 12.0 %copy-start.1 = (f32[1,4,8,1326]{3,2,1,0:T(8,128)S(1)}, f32[1,4,8,1326]{3,2,1,0:T(8,128)}, u32[]{:S(2)}) copy-start(f32[1,4,8,1326]{3,2,1,0:T(8,128)} %param.15) | copy-start | bytes 509188
Sparse Core Ops, SparseCore 0:
  9.6 38.6 all-gather.2
  66.7 34.9 all-gather.4
  113.8 41.0 all-reduce.1
where the time goes:
time: 164 us
  waiting for transfers between devices  101 us (62%)
  other arithmetic  21.4 us (13%)
  matrix products  15 us (9%)
  between operations  13.9 us (8%)
  blocking collectives  10.5 us (6%)
  local copies, waits for them, and re-layouts  1.84 us (1%)
    psum x1, waiting for transfers between devices, local(): section_sum, live_total = lax.psum((section_part, live_part), 'board')  40.3 us
    all_gather x1, waiting for transfers between devices, local(): factor_all = lax.all_gather(factor[None], 'section', axis=0, tiled=True)  36.4 us
    all_gather x1, waiting for transfers between devices, local(): leaf_all = lax.all_gather(weighted[None], 'section', axis=0, tiled=True)  23.9 us
    dot_general x4, matrix products, showdown(): jnp.einsum('rk,hk->rh', flipped, payoff, preferred_element_type=jnp.float32)  15 us
    select_n x8, other arithmetic, climb(): return jnp.where(level_now > section_idx, updated, carried)  10.9 us
    psum x1, blocking collectives, local(): section_sum, live_total = lax.psum((section_part, live_part), 'board')  10.5 us
  transfers between devices with their start and end apart: 3, of which 3 were waited for; matrix products, arithmetic and copies ran while one was open for 3% of the time, Pallas kernels for 0%

commit v1 on v0

--- a/solution.py
+++ b/solution.py
@@ -45,6 +45,16 @@
 
 
 def local(root_reach, frontier_value, regret_stop, regret_go, board_live, board_cards, hand_rank):
+
+    def links_place(d0, my_tile):
+        answer = jnp.concatenate(
+            lax.all_to_all(
+                jnp.stack([my_tile for _ in range(lax.psum(1, "section"))], axis=0), "section", 0, 0
+            ),
+            axis=d0,
+        )
+        return answer
+
     section_idx = lax.axis_index("section")
     players = jnp.arange(2)[:, None, None]
     acting = players == section_idx % 2
@@ -59,7 +69,7 @@
     factor = jnp.where(acting[None], go_prob[:, None], 1.0)
     stop_weight = jnp.where(acting[None], stop_prob[:, None], 1.0)
     root_masked = root_reach[None] * masks[:, None, None, :]
-    factor_all = lax.all_gather(factor[None], "section", axis=0, tiled=True)
+    factor_all = links_place(0, factor[None])
     levels = jnp.arange(factor_all.shape[0])[:, None, None, None, None]
     reach_now = root_masked * jnp.prod(jnp.where(levels < section_idx, factor_all, 1.0), axis=0)
     disjoint = free_pairs()

time: 164 us -> 207 us (1.26)
  waiting for transfers between devices: 101 us -> 127 us
  local copies, waits for them, and re-layouts: 1.84 us -> 8.68 us
  starting transfers between devices: 0.12 us -> 6.58 us
    all_to_all x0 -> x1, waiting for transfers between devices: none -> 64.3 us  [links_place(): lax.all_to_all(jnp.stack([my_tile for _ in range(lax.psum(1, 'section'))]...]
    all_gather x1 -> x0, waiting for transfers between devices: 36.4 us -> none  [local(): factor_all = lax.all_gather(factor[None], 'section', axis=0, tiled=True)]
    all_to_all x0 -> x1, starting transfers between devices: none -> 6.5 us  [links_place(): lax.all_to_all(jnp.stack([my_tile for _ in range(lax.psum(1, 'section'))]...]
    rev x4, local copies, waits for them, and re-layouts: 0.02 us -> 4.05 us  [showdown(): flipped = leaf_reach[::-1].reshape(-1, leaf_reach.shape[-1])]
  transfers between devices with their start and end apart: 3 -> 3, of which waited for: 3 -> 3; matrix products, arithmetic and copies ran while one was open for 3% -> 2% of each run, Pallas kernels for 0% -> 0%
where the time goes in v1:
time: 207 us; the launch traced here: 206 us
  waiting for transfers between devices  127 us (61%)
  other arithmetic  22.5 us (11%)
  matrix products  15.8 us (8%)
  between operations  14.3 us (7%)
  blocking collectives  10.5 us (5%)
  local copies, waits for them, and re-layouts  8.68 us (4%)
  starting transfers between devices  6.58 us (3%)
    all_to_all x1, waiting for transfers between devices, links_place(): lax.all_to_all(jnp.stack([my_tile for _ in range(lax.psum(1, 'section'))]...  64.3 us
    psum x1, waiting for transfers between devices, local(): section_sum, live_total = lax.psum((section_part, live_part), 'board')  39.3 us
    all_gather x1, waiting for transfers between devices, local(): leaf_all = lax.all_gather(weighted[None], 'section', axis=0, tiled=True)  23.8 us
    dot_general x4, matrix products, showdown(): jnp.einsum('rk,hk->rh', flipped, payoff, preferred_element_type=jnp.float32)  15.8 us
    psum x1, blocking collectives, local(): section_sum, live_total = lax.psum((section_part, live_part), 'board')  10.5 us
    select_n x8, other arithmetic, climb(): return jnp.where(level_now > section_idx, updated, carried)  10 us
    all_to_all x1, starting transfers between devices, links_place(): lax.all_to_all(jnp.stack([my_tile for _ in range(lax.psum(1, 'section'))]...  6.5 us
  transfers between devices with their start and end apart: 3, of which 3 were waited for; matrix products, arithmetic and copies ran while one was open for 2% of the time, Pallas kernels for 0%

profile of v1, /device:TPU:0, one launch (start us, length us, event | category | flops | bytes accessed | tf_op | source)
XLA Modules:
  0.0 206.0 jit_solution(17584154837732667624)
XLA Ops:
  7.2 1.0 add_divide_fusion.1
  8.3 0.7 copy-done
  8.9 0.9 broadcast_select_fusion.1
  9.8 1.8 stack.16
  11.6 6.5 %all-to-all-start = ((f32[8,1,4,2,8,1326]{5,4,3,2,1,0:T(8,128)}), f32[8,1,4,2,8,1326]{5,4,3,2,1,0:T(8,128)S(1)}, u32[]{:S(2)}, u32[]{:S(2)}) async-start(f32[8,1,4,2,8,1326]{5,4,3,2,1,0:T(8,128)} %stack.16), calls=%async_computation | async-start | bytes 5767168 | tf_op jit(solution)/shard_map/all_to_all | solution.py:51
  18.5 0.7 fusion.53
  19.1 0.7 slice_reduce_fusion.3
  19.8 64.3 %all-to-all-done = f32[8,1,4,2,8,1326]{5,4,3,2,1,0:T(8,128)S(1)} async-done(((f32[8,1,4,2,8,1326]{5,4,3,2,1,0:T(8,128)}), f32[8,1,4,2,8,1326]{5,4,3,2,1,0:T(8,128)S(1)}, u32[]{:S(2)}, u32[]{:S(2)}) %all-to-all-start) | async-done | bytes 2715680 | tf_op jit(solution)/shard_map/all_to_all | solution.py:51
  84.3 1.0 multiply_multiply_fusion
  85.3 1.7 fusion.46
  87.0 1.4 rev.12
  88.4 1.4 rev.13
  91.0 4.5 %fusion.24 = f32[2,8,1326]{2,1,0:T(8,128)S(1)} fusion(bf16[2,8,1326]{2,1,0:T(8,128)(2,1)} %rev.12, s32[1326]{0:T(1024)} %get-tuple-element.143, s32[1326]{0:T(1024)S(1)} %copy-done.10, s32[1326]{0:T(1024)S(1)} %copy-done.9, bf16[1326]{0:T(1024)(128)(2,1)} %get-tuple-element.139), kind=kOutput, calls=%fused_computation.27 | convolution fusion | flops 91430352 | bytes 145860 | tf_op jit(solution)/shard_map/rk,hk->rh/dot_general | solution.py:43
  95.6 3.7 %fusion.22 = f32[2,8,1326]{2,1,0:T(8,128)S(1)} fusion(bf16[2,8,1326]{2,1,0:T(8,128)(2,1)S(1)} %copy-done.7, s32[1326]{0:T(1024)S(1)} %copy-done.13, s32[1326]{0:T(1024)S(1)} %copy-done.10, s32[1326]{0:T(1024)S(1)} %copy-done.9, bf16[1326]{0:T(1024)(128)(2,1)S(1)} %copy-done.18), kind=kOutput, calls=%fused_computation.26 | convolution fusion | flops 91430352 | bytes 145860 | tf_op jit(solution)/shard_map/rk,hk->rh/dot_general | solution.py:43
  99.4 3.7 %fusion.20 = f32[2,8,1326]{2,1,0:T(8,128)S(1)} fusion(bf16[2,8,1326]{2,1,0:T(8,128)(2,1)S(1)} %copy-done.6, s32[1326]{0:T(1024)S(1)} %copy-done.12, s32[1326]{0:T(1024)S(1)} %copy-done.10, s32[1326]{0:T(1024)S(1)} %copy-done.9, bf16[1326]{0:T(1024)(128)(2,1)S(1)} %copy-done.17), kind=kOutput, calls=%fused_computation.25 | convolution fusion | flops 91430352 | bytes 145860 | tf_op jit(solution)/shard_map/rk,hk->rh/dot_general | solution.py:43
  103.1 3.9 %fusion.18 = f32[2,8,1326]{2,1,0:T(8,128)S(1)} fusion(bf16[2,8,1326]{2,1,0:T(8,128)(2,1)S(1)} %copy-done.5, s32[1326]{0:T(1024)S(1)} %copy-done.11, s32[1326]{0:T(1024)S(1)} %copy-done.10, s32[1326]{0:T(1024)S(1)} %copy-done.9, bf16[1326]{0:T(1024)(128)(2,1)S(1)} %copy-done.16), kind=kOutput, calls=%fused_computation.24 | convolution fusion | flops 91430352 | bytes 145860 | tf_op jit(solution)/shard_map/rk,hk->rh/dot_general | solution.py:43
  107.7 0.9 maximum_multiply_fusion
  109.2 10.5 %psum.15 = f32[]{:T(128)} all-reduce(f32[]{:T(128)} %convert_reduce_fusion), channel_id=1, replica_groups=mesh['section'=8,'board'=4] {'board'}, use_global_device_ids=true, to_apply=%region_9.10 | all-reduce | flops 1 | bytes 8 | tf_op jit(solution)/shard_map/psum | solution.py:97
  119.8 23.8 %all-gather.2.cloned.1.call-done = f32[8,4,2,8,1326]{4,3,2,1,0:T(8,128)} async-done(((f32[1,4,2,8,1326]{4,3,2,1,0:T(8,128)}), f32[8,4,2,8,1326]{4,3,2,1,0:T(8,128)}) %all-gather.2.cloned.1.call-update) | async-done | bytes 2715664 | tf_op jit(solution)/shard_map/all_gather | solution.py:85
  143.6 10.2 %while.15 = (s32[]{:T(128)}, f32[4,2,8,1326]{3,2,1,0:T(8,128)S(1)}, s32[]{:T(128)}, f32[8,4,2,8,1326]{4,3,2,1,0:T(8,128)}, f32[8,4,2,8,1326]{4,3,2,1,0:T(8,128)S...) while((s32[]{:T(128)}, f32[4,2,8,1326]{3,2,1,0:T(8,128)S(1)}, s32[]{:T(128)}, ...), condition=%wide.region_4.5_spmd, body=%wide.region_3.4_spmd.sunk | while | flops 254599 | bytes 1357977 | solution.py:93
  143.6 1.2 fusion.68
  144.9 1.3 fusion.68
  146.1 1.3 fusion.68
  147.4 1.3 fusion.68
  148.7 1.3 fusion.68
  150.0 1.3 fusion.68
  151.3 1.3 fusion.68
  152.5 1.3 fusion.68
  153.8 1.9 multiply_reduce_fusion
  155.8 1.9 fusion.41
  157.6 39.3 %all-reduce.2.cloned.1.call-done = f32[2,8,1326]{2,1,0:T(8,128)} async-done(((f32[2,8,1326]{2,1,0:T(8,128)}), f32[2,8,1326]{2,1,0:T(8,128)}) %all-reduce.2.cloned.1.call-update) | async-done | bytes 84880 | tf_op jit(solution)/shard_map/psum | solution.py:97
  197.0 2.2 %divide_bitcast_fusion = f32[1,2,8,1326]{3,2,1,0:T(8,128)} fusion(f32[2,8,1326]{2,1,0:T(8,128)} %all-reduce.2.cloned.1.call-done, f32[]{:T(128)} %psum.15), kind=kLoop, calls=%fused_computation.67 | loop fusion | flops 21216 | bytes 169732 | tf_op jit(solution)/shard_map/broadcast_in_dim | solution.py:105
  (55 shorter events, 3.2 us)
Async XLA Ops:
  7.2 2.6 %copy-start.14 = (pred[2]{0:T(512)(128)(4,1)}, pred[2]{0:T(512)(128)(4,1)S(1)}, u32[]{:S(2)}) copy-start(pred[2]{0:T(512)(128)(4,1)S(1)} %iota_compare_fusion.1) | copy-start | bytes 10
  8.2 0.7 copy-start
  11.6 6.6 %copy-start.19 = (s32[4,5]{1,0:T(4,128)S(1)}, s32[4,5]{1,0:T(4,128)}, u32[]{:S(2)}) copy-start(s32[4,5]{1,0:T(4,128)} %param.18) | copy-start | bytes 244
  11.6 6.7 %copy-start.9 = (s32[1326]{0:T(1024)S(1)}, s32[1326]{0:T(1024)}, u32[]{:S(2)}) copy-start(s32[1326]{0:T(1024)} %constant.74.clone) | copy-start | bytes 15916
  11.6 6.7 %copy-start.10 = (s32[1326]{0:T(1024)S(1)}, s32[1326]{0:T(1024)}, u32[]{:S(2)}) copy-start(s32[1326]{0:T(1024)} %constant.75.clone) | copy-start | bytes 15916
  11.6 7.5 %copy-start.8 = (s32[4,1326]{1,0:T(4,128)S(1)}, s32[4,1326]{1,0:T(4,128)}, u32[]{:S(2)}) copy-start(s32[4,1326]{1,0:T(4,128)} %param.19) | copy-start | bytes 63652
  11.6 72.4 %all-to-all-start = ((f32[8,1,4,2,8,1326]{5,4,3,2,1,0:T(8,128)}), f32[8,1,4,2,8,1326]{5,4,3,2,1,0:T(8,128)S(1)}, u32[]{:S(2)}, u32[]{:S(2)}) async-start(f32[8,1,4,2,8,1326]{5,4,3,2,1,0:T(8,128)} %stack.16), calls=%async_computation | async-start | bytes 5767168 | tf_op jit(solution)/shard_map/all_to_all | solution.py:51
  18.1 66.2 %copy-start.4 = (f32[2,8,1326]{2,1,0:T(8,128)S(1)}, f32[2,8,1326]{2,1,0:T(8,128)}, u32[]{:S(2)}) copy-start(f32[2,8,1326]{2,1,0:T(8,128)} %param.13) | copy-start | bytes 254596
  18.1 125.4 %all-gather.2.cloned.1.call-start = ((), (), s32[]{:S(2)}) async-start(), calls=%async_computation.1 | async-start | bytes 3244032 | tf_op jit(solution)/shard_map/all_gather | solution.py:85
  91.0 4.5 %copy-start.7 = (bf16[2,8,1326]{2,1,0:T(8,128)(2,1)S(1)}, bf16[2,8,1326]{2,1,0:T(8,128)(2,1)}, u32[]{:S(2)}) copy-start(bf16[2,8,1326]{2,1,0:T(8,128)(2,1)} %rev.13) | copy-start | bytes 127300
  91.0 4.5 %copy-start.13 = (s32[1326]{0:T(1024)S(1)}, s32[1326]{0:T(1024)}, u32[]{:S(2)}) copy-start(s32[1326]{0:T(1024)} %get-tuple-element.144) | copy-start | bytes 15916
  91.0 4.5 %copy-start.18 = (bf16[1326]{0:T(1024)(128)(2,1)S(1)}, bf16[1326]{0:T(1024)(128)(2,1)}, u32[]{:S(2)}) copy-start(bf16[1326]{0:T(1024)(128)(2,1)} %get-tuple-element.142) | copy-start | bytes 7960
  95.6 3.7 %copy-start.6 = (bf16[2,8,1326]{2,1,0:T(8,128)(2,1)S(1)}, bf16[2,8,1326]{2,1,0:T(8,128)(2,1)}, u32[]{:S(2)}) copy-start(bf16[2,8,1326]{2,1,0:T(8,128)(2,1)} %rev.14) | copy-start | bytes 127300
  95.6 3.7 %copy-start.12 = (s32[1326]{0:T(1024)S(1)}, s32[1326]{0:T(1024)}, u32[]{:S(2)}) copy-start(s32[1326]{0:T(1024)} %get-tuple-element.146) | copy-start | bytes 15916
  95.6 3.7 %copy-start.17 = (bf16[1326]{0:T(1024)(128)(2,1)S(1)}, bf16[1326]{0:T(1024)(128)(2,1)}, u32[]{:S(2)}) copy-start(bf16[1326]{0:T(1024)(128)(2,1)} %get-tuple-element.141) | copy-start | bytes 7960
  99.3 7.7 %copy-start.1 = (f32[2,8,1326]{2,1,0:T(8,128)}, f32[2,8,1326]{2,1,0:T(8,128)S(1)}, u32[]{:S(2)}) copy-start(f32[2,8,1326]{2,1,0:T(8,128)S(1)} %fusion.22) | copy-start | bytes 254596
  99.4 3.7 %copy-start.5 = (bf16[2,8,1326]{2,1,0:T(8,128)(2,1)S(1)}, bf16[2,8,1326]{2,1,0:T(8,128)(2,1)}, u32[]{:S(2)}) copy-start(bf16[2,8,1326]{2,1,0:T(8,128)(2,1)} %rev.15) | copy-start | bytes 127300
  99.4 3.7 %copy-start.11 = (s32[1326]{0:T(1024)S(1)}, s32[1326]{0:T(1024)}, u32[]{:S(2)}) copy-start(s32[1326]{0:T(1024)} %get-tuple-element.145) | copy-start | bytes 15916
  99.4 3.7 %copy-start.16 = (bf16[1326]{0:T(1024)(128)(2,1)S(1)}, bf16[1326]{0:T(1024)(128)(2,1)}, u32[]{:S(2)}) copy-start(bf16[1326]{0:T(1024)(128)(2,1)} %get-tuple-element.140) | copy-start | bytes 7960
  103.1 3.9 %copy-start.2 = (f32[2,8,1326]{2,1,0:T(8,128)}, f32[2,8,1326]{2,1,0:T(8,128)S(1)}, u32[]{:S(2)}) copy-start(f32[2,8,1326]{2,1,0:T(8,128)S(1)} %fusion.20) | copy-start | bytes 254596
  103.1 4.5 %copy-start.15 = (pred[2]{0:T(512)(128)(4,1)S(1)}, pred[2]{0:T(512)(128)(4,1)}, u32[]{:S(2)}) copy-start(pred[2]{0:T(512)(128)(4,1)} %copy-done.14) | copy-start | bytes 10
  103.1 5.5 %copy-start.20 = (s32[4]{0:T(128)S(1)}, s32[4]{0:T(128)}, u32[]{:S(2)}) copy-start(s32[4]{0:T(128)} %param.17) | copy-start | bytes 52
  107.0 0.6 copy-start.3
  108.5 88.4 %all-reduce.2.cloned.1.call-start = ((), (), s32[]{:S(2)}) async-start(), calls=%async_computation.2 | async-start | bytes 180224 | tf_op jit(solution)/shard_map/psum | solution.py:97
Sparse Core Ops, SparseCore 0:
  108.7 34.8 all-gather.1
  155.9 41.0 all-reduce.1
